TPU v7x, 32 devices: a whole 2x2x4 slice. The times are simulated.
32 devices in a mesh: dp: 4 (over y, core), fsdp: 8 (over z, x).
Axes of the slice: x: 2, y: 2, z: 4, core: 2. Of those that a mesh axis runs over, the one named last changes fastest.
Arguments:
- data_samples: bfloat16 [512, 4096], P('dp', 'fsdp'), may hold values from -6 to 6
- negative_start: float32 [512, 4096], P('dp', 'fsdp'), may hold values from -6 to 6
- langevin_noise: float32 [4, 512, 4096], P(None, 'dp', 'fsdp'), may hold values from -6 to 6
- first_weight: bfloat16 [4096, 4096], P('fsdp'), may hold values from -0.09375 to 0.09375
- second_weight: bfloat16 [4096, 4096], P('fsdp'), may hold values from -0.09375 to 0.09375
- readout: float32 [4096], P('fsdp'), may hold values from -480 to 480
Outputs:
- first_grad: float32 [4096, 4096], P('fsdp', 'dp')
- second_grad: float32 [4096, 4096], P('fsdp', 'dp')
- energy_gap: float32 [], replicated
All inputs are finite; a program needn't handle non-finite values.
Results may differ from a plain program's by a relative error of at most 0.014.
Values may be sent and summed in bfloat16 or wider, within the bound.
A program may use at most 64 MiB of HBM per device.

v0:
```python
import functools

import jax
import jax.numpy as jnp
from jax import lax
from jax.experimental import pallas as pl
from jax.experimental.pallas import tpu as pltpu
from jax.sharding import PartitionSpec as P

MESH = pl.DeviceIdType.MESH
BF16 = jnp.bfloat16
F32 = jnp.float32


def inner_of(n):
    return max(i for i in range(1, n + 1) if n % i == 0 and i * i <= n)


def folded(values):
    rows, columns = values.shape
    tall = values.reshape(rows // 8, 8, columns).sum(axis=0)
    out = tall[:, :128]
    for at in range(128, columns, 128):
        out += tall[:, at : at + 128]
    return out


def kernel(
    n, X, dpn, steps, S,
    data_ref, start_ref, noise_ref, w1_ref, w2_ref, read_ref,
    raw1_ref, raw2_ref, stat_ref,
    state, s_a, r_a, s_b, r_b, acc, ag_data, ag_neg, rows_all, hid_all, g_all, own_stat, got_stat,
    sem_as, sem_ar, sem_bs, sem_br, sem_zs, sem_zr, sem_xs, sem_xr, sem_ds, sem_dr, sem_ts, sem_tr,
):
    Z = n // X
    q = n // dpn
    C = w1_ref.shape[1] // n
    height = data_ref.shape[0] // S
    me = lax.axis_index("fsdp")
    dpi = lax.axis_index("dp")
    z, x = me // X, me % X

    def dest(oz, ox):
        return ((z + oz) % Z) * X + (x + ox) % X

    def source(oz, ox):
        return ((z + Z - oz) % Z) * X + (x + X - ox) % X

    def dp_dest(o):
        return (dpi + o) % dpn

    def cols(at):
        return pl.ds(pl.multiple_of(at * C, C), C)

    def send(src, dst, ssem, rsem, axis, peer):
        return pltpu.make_async_remote_copy(
            src_ref=src, dst_ref=dst, send_sem=ssem, recv_sem=rsem,
            device_id={axis: peer}, device_id_type=MESH,
        )

    partners = (
        [("fsdp", dest(0, ox)) for ox in range(1, X)]
        + [("fsdp", dest(oz, 0)) for oz in range(1, Z)]
        + [("dp", dp_dest(o)) for o in range(1, dpn)]
    )
    barrier = pltpu.get_barrier_semaphore()
    for axis, peer in partners:
        pl.semaphore_signal(barrier, inc=1, device_id={axis: peer}, device_id_type=MESH)
    pl.semaphore_wait(barrier, len(partners))

    def a_copy(s, j, oz, ox):
        return send(
            s_a.at[s, j, oz, ox - 1], r_a.at[s, j, oz, ox - 1],
            sem_as.at[s, j, oz, ox - 1], sem_ar.at[s, j, oz, ox - 1], "fsdp", dest(0, ox),
        )

    def b_copy(s, j, oz):
        return send(
            s_b.at[s, j, oz - 1], r_b.at[s, j, oz - 1],
            sem_bs.at[s, j, oz - 1], sem_br.at[s, j, oz - 1], "fsdp", dest(oz, 0),
        )

    def z_copy(s, j, oz, buf, at):
        ref = buf.at[s, j, at]
        return send(ref, ref, sem_zs.at[s, j, oz - 1], sem_zr.at[s, j, oz - 1], "fsdp", dest(oz, 0))

    def x_copy(s, j, oz, ox, buf, at):
        ref = buf.at[s, j, at]
        return send(
            ref, ref, sem_xs.at[s, j, oz, ox - 1], sem_xr.at[s, j, oz, ox - 1], "fsdp", dest(0, ox)
        )

    def scatter_open(s, j, lhs, w_ref):
        order = list(range(1, Z)) + [0]
        for oz in order:
            for ox in range(1, X):
                s_a[s, j, oz, ox - 1] = jnp.dot(
                    lhs, w_ref[:, cols(dest(oz, ox))], preferred_element_type=F32
                ).astype(BF16)
                a_copy(s, j, oz, ox).start()
        for oz in order:
            acc[s, oz] = jnp.dot(lhs, w_ref[:, cols(dest(oz, 0))], preferred_element_type=F32)

    def joined(s, j, oz):
        total = acc[s, oz]
        for ox in range(1, X):
            a_copy(s, j, oz, ox).wait_recv()
            total += r_a[s, j, oz, ox - 1].astype(F32)
        return total

    def scatter_join(s, j):
        for oz in range(1, Z):
            s_b[s, j, oz - 1] = joined(s, j, oz).astype(BF16)
            b_copy(s, j, oz).start()

    def scatter_close(s, j):
        total = joined(s, j, 0)
        for oz in range(1, Z):
            b_copy(s, j, oz).wait_recv()
            total += r_b[s, j, oz - 1].astype(F32)
        return total

    def scatter_settle(s, j):
        for oz in range(Z):
            for ox in range(1, X):
                a_copy(s, j, oz, ox).wait_send()
        for oz in range(1, Z):
            b_copy(s, j, oz).wait_send()

    def gather_open(s, j, buf):
        for oz in range(1, Z):
            z_copy(s, j, oz, buf, me).start()
        for ox in range(1, X):
            x_copy(s, j, 0, ox, buf, me).start()

    def block(s, j, buf, at, w_ref):
        return lax.dot_general(
            buf[s, j, at], w_ref[:, cols(at)], (((1,), (1,)), ((), ())), preferred_element_type=F32
        )

    def gather_forward(s, j, buf, w_ref):
        total = None if w_ref is None else block(s, j, buf, me, w_ref)
        for oz in range(1, Z):
            at = source(oz, 0)
            z_copy(s, j, oz, buf, at).wait_recv()
            for ox in range(1, X):
                x_copy(s, j, oz, ox, buf, at).start()
            if w_ref is not None:
                total += block(s, j, buf, at, w_ref)
        return total

    def gather_close(s, j, buf, w_ref, total):
        for oz in range(Z):
            for ox in range(1, X):
                at = source(oz, ox)
                x_copy(s, j, oz, ox, buf, at).wait_recv()
                if w_ref is not None:
                    total += block(s, j, buf, at, w_ref)
        return total

    def gather_settle(s, j, buf):
        for oz in range(1, Z):
            z_copy(s, j, oz, buf, me).wait_send()
        for oz in range(Z):
            for ox in range(1, X):
                x_copy(s, j, oz, ox, buf, source(oz, 0)).wait_send()

    def stages(s, u, sign, buf, keep, after, w_back):
        scatter_join(s, 0)
        yield
        a1 = scatter_close(s, 0)
        s1 = jax.nn.sigmoid(a1)
        hidden = (a1 * s1).astype(BF16)
        slope_1 = s1 * (1.0 + a1 * (1.0 - s1))
        scatter_open(s, 1, hidden, w2_ref)
        scatter_settle(s, 0)
        yield
        scatter_join(s, 1)
        yield
        a2 = scatter_close(s, 1)
        s2 = jax.nn.sigmoid(a2)
        buf[s, 0, me] = (sign * read_ref[...] * (s2 * (1.0 + a2 * (1.0 - s2)))).astype(BF16)
        gather_open(s, 0, buf)
        scatter_settle(s, 1)
        yield
        total = gather_forward(s, 0, buf, w2_ref)
        yield
        back = gather_close(s, 0, buf, w2_ref, total)
        buf[s, 1, me] = (back * slope_1).astype(BF16)
        gather_open(s, 1, buf)
        keep(s, 0, u, hidden, a2 * s2)
        yield
        total = gather_forward(s, 1, buf, w_back)
        yield
        moved = gather_close(s, 1, buf, w_back, total)
        keep(s, 1, u, hidden, None)
        gather_settle(s, 0, buf)
        gather_settle(s, 1, buf)
        after(s, moved)

    def interleave(passes):
        passes = list(passes)
        while passes:
            passes = [p for p in passes if next(p, passes) is not passes]

    def dp_ref(half, kind, d, s):
        if kind == 0:
            return rows_all.at[half, d, s]
        if kind == 1:
            return hid_all.at[half, d, s]
        return g_all.at[half, (kind - 2) // q, (kind - 2) % q, d, s]

    def dp_copy(half, kind, o, s, src, d):
        return send(
            src, dp_ref(half, kind, d, s), sem_ds.at[half, kind, o - 1, s],
            sem_dr.at[half, kind, o - 1, s], "dp", dp_dest(o),
        )

    def dp_copies(half, buf, s, stage):
        kinds = ([0, 1] if stage == 0 else []) + [2 + stage * q + k for k in range(q)]
        for kind in kinds:
            for o in range(1, dpn):
                if kind < 2:
                    own = dp_ref(half, kind, dpi, s)
                else:
                    own = buf.at[s, stage, dp_dest(o) * q + (kind - 2) % q]
                yield dp_copy(half, kind, o, s, own, dpi)

    def exchange(half, buf, s, stage, u, hidden, silu_2):
        if stage == 0:
            rows_all[half, dpi, s] = u
            hid_all[half, dpi, s] = hidden
            energy = folded(read_ref[...] * silu_2)
            if half == 0 and s == 0:
                own_stat[0] = energy
            else:
                own_stat[0] = own_stat[0] + energy if half == 0 else own_stat[0] - energy
        for k in range(q):
            g_all[half, stage, k, dpi, s] = buf[s, stage, dpi * q + k]
        for copy in dp_copies(half, buf, s, stage):
            copy.start()

    def nothing(*args):
        return None

    def rows_of(s):
        return pl.ds(s * height, height)

    def opened(s, *args):
        scatter_open(s, 0, state[rows_of(s), :].astype(BF16), w1_ref)

    streams = range(S)
    for s in streams:
        scatter_open(s, 0, data_ref[rows_of(s), :], w1_ref)
    state[...] = start_ref[...]
    interleave(
        stages(
            s, data_ref[rows_of(s), :], 1.0, ag_data, functools.partial(exchange, 0, ag_data), opened, None
        )
        for s in streams
    )

    def langevin(step, carry):
        def after(s, moved):
            at = rows_of(s)
            state[at, :] = state[at, :] - 0.005 * moved + 0.1 * noise_ref[step, at, :]
            opened(s)

        interleave(stages(s, None, 1.0, ag_neg, nothing, after, w1_ref) for s in streams)
        return carry

    lax.fori_loop(0, steps, langevin, 0)

    def contract(left, right):
        return lax.dot_general(
            left.reshape(-1, left.shape[-1]), right.reshape(-1, right.shape[-1]),
            (((0,), (0,)), ((), ())), preferred_element_type=F32,
        )

    def arrived(half, kinds):
        for s in streams:
            for kind in kinds:
                for o in range(1, dpn):
                    at = (dpi + dpn - o) % dpn
                    dp_copy(half, kind, o, s, dp_ref(half, kind, at, s), at).wait_recv()

    def gradients():
        for _ in range(6):
            yield
        arrived(0, range(2 + 2 * q))
        for g, left, out_ref in ((1, rows_all, raw1_ref), (0, hid_all, raw2_ref)):
            for k in range(q):
                out_ref[:, k * C : (k + 1) * C] = contract(left[0], g_all[0, g, k])

    interleave(
        [
            stages(
                s, state[rows_of(s), :].astype(BF16), -1.0, ag_neg,
                functools.partial(exchange, 1, ag_neg), nothing, None,
            )
            for s in streams
        ]
        + [gradients()]
    )

    squares = jnp.zeros((8, 128), F32)
    for g, left, out_ref in ((0, hid_all, raw2_ref), (1, rows_all, raw1_ref)):
        arrived(1, ([0, 1] if g == 0 else []) + [2 + g * q + k for k in range(q)])
        for k in range(q):
            at = slice(k * C, (k + 1) * C)
            raw = out_ref[:, at] + contract(left[1], g_all[1, g, k])
            out_ref[:, at] = raw
            squares += folded(raw * raw)
    own_stat[1] = squares

    for half, buf in ((0, ag_data), (1, ag_neg)):
        for s in streams:
            for stage in range(2):
                for copy in dp_copies(half, buf, s, stage):
                    copy.wait_send()

    base = 0
    for axis, count, peer in (
        ("fsdp", X, lambda o: dest(0, o)), ("fsdp", Z, lambda o: dest(o, 0)), ("dp", dpn, dp_dest),
    ):
        copies = []
        for o in range(1, count):
            at = base + o - 1
            copy = send(own_stat, got_stat.at[at], sem_ts.at[at], sem_tr.at[at], axis, peer(o))
            copy.start()
            copies.append(copy)
        total = own_stat[...]
        for o, copy in enumerate(copies):
            copy.wait()
            total += got_stat[base + o]
        own_stat[...] = total
        base += count - 1
    stat_ref[...] = own_stat[...]


def solution(mesh):
    n, dpn = mesh.shape["fsdp"], mesh.shape["dp"]
    X = inner_of(n)
    Z = n // X
    q = n // dpn

    def local(data, start, noise, w1, w2, readout):
        R, K = start.shape
        H = w1.shape[1]
        C = H // n
        steps = noise.shape[0]
        S = 2 if R % 32 == 0 else 1
        h = R // S
        vmem = pl.BlockSpec(memory_space=pltpu.VMEM)
        dma = pltpu.SemaphoreType.DMA
        kinds = 2 + 2 * q
        peers = (X - 1) + (Z - 1) + (dpn - 1)
        raw1, raw2, stat = pl.pallas_call(
            functools.partial(kernel, n, X, dpn, steps, S),
            name="contrastive",
            out_shape=(
                jax.ShapeDtypeStruct((K, q * C), F32),
                jax.ShapeDtypeStruct((C, q * C), F32),
                jax.ShapeDtypeStruct((2, 8, 128), F32),
            ),
            in_specs=[vmem] * 6,
            out_specs=(vmem,) * 3,
            scratch_shapes=[
                pltpu.VMEM((R, K), F32),
                pltpu.VMEM((S, 2, Z, X - 1, h, C), BF16),
                pltpu.VMEM((S, 2, Z, X - 1, h, C), BF16),
                pltpu.VMEM((S, 2, Z - 1, h, C), BF16),
                pltpu.VMEM((S, 2, Z - 1, h, C), BF16),
                pltpu.VMEM((S, Z, h, C), F32),
                pltpu.VMEM((S, 2, n, h, C), BF16),
                pltpu.VMEM((S, 2, n, h, C), BF16),
                pltpu.VMEM((2, dpn, S, h, K), BF16),
                pltpu.VMEM((2, dpn, S, h, C), BF16),
                pltpu.VMEM((2, 2, q, dpn, S, h, C), BF16),
                pltpu.VMEM((2, 8, 128), F32),
                pltpu.VMEM((peers, 2, 8, 128), F32),
                dma((S, 2, Z, X - 1)), dma((S, 2, Z, X - 1)),
                dma((S, 2, Z - 1)), dma((S, 2, Z - 1)),
                dma((S, 2, Z - 1)), dma((S, 2, Z - 1)),
                dma((S, 2, Z, X - 1)), dma((S, 2, Z, X - 1)),
                dma((2, kinds, dpn - 1, S)), dma((2, kinds, dpn - 1, S)),
                dma((peers,)), dma((peers,)),
            ],
            compiler_params=pltpu.CompilerParams(
                collective_id=0, has_side_effects=True, vmem_limit_bytes=60 * 1024 * 1024
            ),
        )(data, start, noise, w1, w2, readout.reshape(1, C))
        sums = jnp.sum(stat, axis=(1, 2))
        energy_gap = sums[0] / (R * dpn * 80.0 * jnp.sqrt(jnp.float32(H)))
        scale = jnp.sqrt(sums[1] / (2.0 * (K * n) * H) + 1e-06)
        return raw1 / scale, raw2 / scale, energy_gap

    in_specs = (
        P("dp", "fsdp"),
        P("dp", "fsdp"),
        P(None, "dp", "fsdp"),
        P("fsdp", None),
        P("fsdp", None),
        P("fsdp"),
    )
    out_specs = (P("fsdp", "dp"), P("fsdp", "dp"), P())
    return jax.shard_map(local, mesh=mesh, in_specs=in_specs, out_specs=out_specs, check_vma=False)
```

profile of v0, /device:TPU:0, one launch (start us, length us, event | category | flops | bytes accessed | tf_op | source)
XLA Modules:
  0.0 376.9 jit_solution(4593319012607745427)
XLA Ops:
  0.6 367.3 %contrastive.1 = (f32[512,1024]{1,0:T(8,128)}, f32[512,1024]{1,0:T(8,128)}, f32[2,8,128]{2,1,0:T(8,128)}) custom-call(bf16[128,512]{1,0:T(8,128)(2,1)} %data_ref.1, f32[128,512]{1,0:T(8,128)} %start_ref.1, f32[4,128,512]{2,1,0:T(8,128)} %noise_ref.1, bf16[512,4096]{1,0:T(8,128)(2,1)} %w1_ref.1, bf16[512,4096]{1,0:T(8,128)(2,1)} %w2_ref.1, f32[1,512]{1,0:T(1,128)} %bitcast.3), custom_call_target="tpu_custom_call" | custom-call | tf_op jit(solution)/shard_map/contrastive/pallas_call | solution.py:358
  368.0 0.8 reduce_sum.9
  368.8 0.6 fusion
  370.7 5.1 %broadcast_divide_fusion = (f32[512,1024]{1,0:T(8,128)}, f32[512,1024]{1,0:T(8,128)}) fusion(f32[512,1024]{1,0:T(8,128)} %get-tuple-element.8, f32[]{:T(128)} %bitcast.1, f32[512,1024]{1,0:T(8,128)} %get-tuple-element.6), kind=kLoop, calls=%fused_computation | loop fusion | flops 1048576 | bytes 8388612 | tf_op jit(solution)/shard_map/div | solution.py:396
where the time goes:
time: 377 us
  Pallas kernels  367 us (97%)
  other arithmetic  5.86 us (2%)
    pallas_call x1, Pallas kernels, local(): pl.pallas_call(functools.partial(kernel, n, X, dpn, steps, S), name='cont...  367 us

commit v1 on v0

v1 whole, which is shorter than its diff:
```python
import functools

import jax
import jax.numpy as jnp
from jax import lax
from jax.experimental import pallas as pl
from jax.experimental.pallas import tpu as pltpu
from jax.sharding import PartitionSpec as P

MESH = pl.DeviceIdType.MESH
BF16 = jnp.bfloat16
F32 = jnp.float32
PIECES = 4


def inner_of(n):
    return max(i for i in range(1, n + 1) if n % i == 0 and i * i <= n)


def folded(values):
    rows, columns = values.shape
    tall = values.reshape(rows // 8, 8, columns).sum(axis=0)
    out = tall[:, :128]
    for at in range(128, columns, 128):
        out += tall[:, at : at + 128]
    return out


def kernel(
    n, X, dpn, steps, S,
    data_ref, start_ref, noise_in, w1_ref, w2_ref, read_ref,
    raw1_ref, raw2_ref, stat_ref,
    wm1, wm2, state, noise, u_own, hid, slope_1, acc, tot, read_all,
    s_a, r_a, s_b, r_b, buf, rows_all, hid_all, g_all, energy, own_stat, got_stat,
    sem_l, sem_is, sem_ir, sem_rs, sem_rr, sem_wzs, sem_wzr, sem_wys, sem_wyr, sem_wcs, sem_wcr,
    sem_as, sem_ar, sem_bs, sem_br, sem_zs, sem_zr, sem_xs, sem_xr, sem_ds, sem_dr, sem_ts, sem_tr,
):
    Z = n // X
    K = Z // 2
    Y = dpn // 2
    T = 2 * S
    q = n // dpn
    C = w1_ref.shape[0]
    H = w1_ref.shape[1]
    h = state.shape[1]
    slice_rows = C // dpn
    piece = H // PIECES
    me = lax.axis_index("fsdp")
    dpi = lax.axis_index("dp")
    z, x = me // X, me % X
    k, a = z // 2, z % 2
    y, c = dpi // 2, dpi % 2
    other = 1 - a
    self_at = k * X + x

    def device(kd, ad, xd):
        return (kd * 2 + ad) * X + xd

    def x_peer(ox):
        return device(k, a, (x + ox) % X)

    def k_peer(ok):
        return device((k + ok) % K, a, x)

    def z_peer(oz):
        return ((z + oz) % Z) * X + x

    def dp_peer(o):
        return (dpi + o) % dpn

    def half_cols(at):
        return pl.ds(pl.multiple_of(at * C, C), C)

    def shard_cols(kd, i, xd):
        return pl.ds(pl.multiple_of(device(kd, i, xd) * C, C), C)

    def send(src, dst, ssem, rsem, peer):
        return pltpu.make_async_remote_copy(
            src_ref=src, dst_ref=dst, send_sem=ssem, recv_sem=rsem, device_id=peer, device_id_type=MESH
        )

    def fetch(src, dst, sem):
        return pltpu.make_async_copy(src, dst, sem)

    offsets = [(oa, od) for oa in range(2) for od in range(dpn) if (oa, od) != (0, 0)]

    def swap_peer(oa, od):
        return {"fsdp": device(k, (a + oa) % 2, x), "dp": dp_peer(od)}

    partners = (
        [{"fsdp": x_peer(ox)} for ox in range(1, X)]
        + [{"fsdp": z_peer(oz)} for oz in range(1, Z)]
        + [swap_peer(oa, od) for oa, od in offsets if od]
    )
    barrier = pltpu.get_barrier_semaphore()
    for peer in partners:
        pl.semaphore_signal(barrier, inc=1, device_id=peer, device_id_type=MESH)
    pl.semaphore_wait(barrier, len(partners))

    partner = {"fsdp": device(k, other, x)}

    def rows_in(half, s):
        return pl.ds(pl.multiple_of((half * S + s) * h, h), h)

    def pieces_in(kind, s, half, slot):
        if kind == 0:
            return data_ref.at[rows_in(half, s), :], u_own.at[S + s, :, half_cols(slot)]
        if kind == 1:
            return start_ref.at[rows_in(half, s), :], state.at[s, :, half_cols(slot)]
        return noise_in.at[:, rows_in(half, s), :], noise.at[:, s, :, half_cols(slot)]

    def keep_in(kind, s):
        src, dst = pieces_in(kind, s, a, a)
        return fetch(src, dst, sem_l.at[kind * S + s])

    def give_in(kind, s, slot):
        src, dst = pieces_in(kind, s, other, slot)
        return send(src, dst, sem_is.at[kind, s], sem_ir.at[kind, s], partner)

    def read_copy(oz, at):
        return send(read_ref, read_all.at[at], sem_rs.at[oz - 1], sem_rr.at[oz - 1], {"fsdp": z_peer(oz)})

    weights = ((w1_ref, wm1), (w2_ref, wm2))

    def keep_w(w):
        src, dst = weights[w]
        return fetch(src, dst.at[half_cols(a), :], sem_l.at[3 * S + w])

    def w_rows(slot, d):
        return pl.ds(pl.multiple_of(slot * C + d * slice_rows, slice_rows), slice_rows)

    def w_cols(p):
        return pl.ds(p * piece, piece)

    def wz_copy(w, p, slot):
        src, dst = weights[w]
        return send(
            src.at[w_rows(0, dpi), w_cols(p)], dst.at[w_rows(slot, dpi), w_cols(p)],
            sem_wzs.at[w, p], sem_wzr.at[w, p], partner,
        )

    def wy_copy(w, p, o, d):
        ref = weights[w][1].at[w_rows(other, d), w_cols(p)]
        return send(
            ref, ref, sem_wys.at[w, p, o - 1], sem_wyr.at[w, p, o - 1], {"dp": ((y + o) % Y) * 2 + c}
        )

    def wc_copy(w, p, o, d):
        ref = weights[w][1].at[w_rows(other, d), w_cols(p)]
        return send(ref, ref, sem_wcs.at[w, p, o], sem_wcr.at[w, p, o], {"dp": y * 2 + 1 - c})

    def y_source(o):
        return (y + Y - o) % Y

    def weight_steps(w):
        for p in range(PIECES + 1):
            if p < PIECES:
                wz_copy(w, p, other).wait_recv()
                for o in range(1, Y):
                    wy_copy(w, p, o, dpi).start()
                wc_copy(w, p, 0, dpi).start()
            if p:
                for o in range(1, Y):
                    d = y_source(o) * 2 + c
                    wy_copy(w, p - 1, o, d).wait_recv()
                    wc_copy(w, p - 1, o, d).start()
            yield
        for p in range(PIECES):
            for o in range(Y):
                wc_copy(w, p, o, y_source(o) * 2 + 1 - c).wait_recv()
        keep_w(w).wait()

    def weight_settle(w):
        for p in range(PIECES):
            wz_copy(w, p, a).wait_send()
            for o in range(1, Y):
                wy_copy(w, p, o, dpi).wait_send()
            for o in range(Y):
                wc_copy(w, p, o, dpi).wait_send()

    def a_copy(s, j, ok, ox):
        return send(
            s_a.at[s, j, ok, ox - 1], r_a.at[s, j, ok, ox - 1],
            sem_as.at[s, j, ok, ox - 1], sem_ar.at[s, j, ok, ox - 1], {"fsdp": x_peer(ox)},
        )

    def b_copy(s, j, ok, part):
        at = 0 if j == 0 else 1 + part
        return send(
            s_b.at[s, ok - 1 if j == 0 else K - 1 + part], r_b.at[s, ok - 1, at],
            sem_bs.at[s, ok - 1, at], sem_br.at[s, ok - 1, at], {"fsdp": k_peer(ok)},
        )

    order = list(range(1, K)) + [0]

    def two_dots(lhs, w, kd, xd):
        return [
            jnp.dot(lhs, w[:, shard_cols(kd, i, xd)], preferred_element_type=F32) for i in range(2)
        ]

    def scatter_open(s, j, lhs, w):
        for ok in order:
            for ox in range(1, X):
                for i, part in enumerate(two_dots(lhs, w, (k + ok) % K, (x + ox) % X)):
                    s_a[s, j, ok, ox - 1, :, i * C : (i + 1) * C] = part.astype(BF16)
                a_copy(s, j, ok, ox).start()
        for ok in order:
            for i, part in enumerate(two_dots(lhs, w, (k + ok) % K, x)):
                acc[s, ok, :, i * C : (i + 1) * C] = part

    def joined(s, j, ok):
        total = acc[s, ok]
        for ox in range(1, X):
            a_copy(s, j, ok, ox).wait_recv()
            total += r_a[s, j, ok, ox - 1].astype(F32)
        return total

    def open_1(s):
        scatter_open(s, 0, u_own[s], wm1)

    def join_1(s):
        for ok in range(1, K):
            s_b[s, ok - 1] = joined(s, 0, ok).astype(BF16)
            b_copy(s, 0, ok, 0).start()

    def close_1(s):
        a1 = joined(s, 0, 0)
        for ok in range(1, K):
            b_copy(s, 0, ok, 0).wait_recv()
            a1 += r_b[s, ok - 1, 0].astype(F32)
        s1 = jax.nn.sigmoid(a1)
        hid[s] = (a1 * s1).astype(BF16)
        slope_1[s] = s1 * (1.0 + a1 * (1.0 - s1))
        scatter_open(s, 1, hid[s], wm2)

    def join_2(s):
        for ok in order:
            total = joined(s, 1, ok)
            acc[s, ok] = total
            s_b[s, K - 1 + ok] = total.astype(BF16)
            for to in range(1, K):
                b_copy(s, 1, to, ok).start()

    def x_copy(s, stage, ok, ox, at):
        ref = buf.at[s, stage, at]
        return send(
            ref, ref, sem_xs.at[s, stage, ok, ox - 1], sem_xr.at[s, stage, ok, ox - 1], {"fsdp": x_peer(ox)}
        )

    def z_copy(s, ok, at):
        ref = buf.at[s, 1, at]
        return send(ref, ref, sem_zs.at[s, ok - 1], sem_zr.at[s, ok - 1], {"fsdp": k_peer(ok)})

    def block(s, stage, kd, xd, w):
        total = None
        for i in range(2):
            part = lax.dot_general(
                buf[s, stage, kd * X + xd, :, i * C : (i + 1) * C], w[:, shard_cols(kd, i, xd)],
                (((1,), (1,)), ((), ())), preferred_element_type=F32,
            )
            total = part if total is None else total + part
        return total

    def close_2(s, sign):
        for ok in order:
            kd = (k + ok) % K
            a2 = acc[s, ok]
            for frm in range(1, K):
                part = (ok + frm) % K
                b_copy(s, 1, frm, part).wait_recv()
                a2 += r_b[s, frm - 1, 1 + part].astype(F32)
            gain = jnp.concatenate([read_all[kd * 2], read_all[kd * 2 + 1]], axis=1)
            s2 = jax.nn.sigmoid(a2)
            buf[s, 0, kd * X + x] = (sign * gain * (s2 * (1.0 + a2 * (1.0 - s2)))).astype(BF16)
            for ox in range(1, X):
                x_copy(s, 0, ok, ox, kd * X + x).start()
            if ok == 0:
                energy[s] = folded(gain * (a2 * s2))
        total = None
        for ok in order:
            part = block(s, 0, (k + ok) % K, x, wm2)
            total = part if total is None else total + part
        tot[s] = total

    def back_2(s):
        total = tot[s]
        for ok in order:
            for ox in range(1, X):
                kd, xd = (k + ok) % K, (x + X - ox) % X
                x_copy(s, 0, ok, ox, kd * X + xd).wait_recv()
                total += block(s, 0, kd, xd, wm2)
        buf[s, 1, self_at] = (total * slope_1[s]).astype(BF16)
        for ok in range(1, K):
            z_copy(s, ok, self_at).start()
        for ox in range(1, X):
            x_copy(s, 1, 0, ox, self_at).start()

    def forward_1(s, moving):
        if moving:
            total = block(s, 1, k, x, wm1)
        for ok in range(1, K):
            kd = (k + K - ok) % K
            z_copy(s, ok, kd * X + x).wait_recv()
            for ox in range(1, X):
                x_copy(s, 1, ok, ox, kd * X + x).start()
            if moving:
                total += block(s, 1, kd, x, wm1)
        if moving:
            tot[s] = total

    def back_1(s, moving):
        if moving:
            total = tot[s]
        for ok in range(K):
            for ox in range(1, X):
                kd, xd = (k + K - ok) % K, (x + X - ox) % X
                x_copy(s, 1, ok, ox, kd * X + xd).wait_recv()
                if moving:
                    total += block(s, 1, kd, xd, wm1)
        if moving:
            return total

    def settle(s):
        for j in range(2):
            for ok in range(K):
                for ox in range(1, X):
                    a_copy(s, j, ok, ox).wait_send()
                    x_copy(s, j, ok, ox, self_at).wait_send()
        for ok in range(1, K):
            b_copy(s, 0, ok, 0).wait_send()
            for part in range(K):
                b_copy(s, 1, ok, part).wait_send()
            z_copy(s, ok, self_at).wait_send()

    def place(half, kind, p, s):
        if kind == 0:
            return rows_all.at[half, p, s]
        if kind == 1:
            return hid_all.at[half, p, s]
        return g_all.at[half, (kind - 2) // q, (kind - 2) % q, p, s]

    def source(half, kind, s, ad, dd):
        at = s if half else S + s
        if kind == 0:
            return u_own.at[at, :, half_cols(ad)]
        if kind == 1:
            return hid.at[at, :, half_cols(ad)]
        stage, i = (kind - 2) // q, (kind - 2) % q
        shard = dd * q + i
        zd, xd = shard // X, shard % X
        return buf.at[at, stage, (zd // 2) * X + xd, :, half_cols(zd % 2)]

    mine = a * dpn + dpi

    def swap(half, kind, e, s, p):
        oa, od = offsets[e]
        return send(
            source(half, kind, s, (a + oa) % 2, dp_peer(od)), place(half, kind, p, s),
            sem_ds.at[half, kind, e, s], sem_dr.at[half, kind, e, s], swap_peer(oa, od),
        )

    def exchange(half, kinds, s):
        for kind in kinds:
            for e in range(len(offsets)):
                swap(half, kind, e, s, mine).start()
        for kind in kinds:
            place(half, kind, mine, s)[...] = source(half, kind, s, a, dpi)[...]

    def arrived(half, kinds):
        def one(s):
            for kind in kinds:
                for e, (oa, od) in enumerate(offsets):
                    p = ((a + oa) % 2) * dpn + (dpi + dpn - od) % dpn
                    swap(half, kind, e, s, p).wait_recv()

        each(0, S, one)

    def exchange_settle(half):
        def one(s):
            for kind in range(2 + 2 * q):
                for e in range(len(offsets)):
                    swap(half, kind, e, s, mine).wait_send()

        each(0, S, one)

    def each(low, high, stage, *args):
        def body(s, carry):
            stage(s, *args)
            return carry

        lax.fori_loop(low, high, body, 0)

    first_kinds, last_kinds = [2 + i for i in range(q)], [2 + q + i for i in range(q)]

    for s in range(S):
        give_in(1, s, a).start()
        give_in(0, s, a).start()
    for w in range(2):
        for p in range(PIECES):
            wz_copy(w, p, a).start()
    for oz in range(1, Z):
        read_copy(oz, z).start()
    for s in range(S):
        keep_in(1, s).start()
        keep_in(0, s).start()
    for w in range(2):
        keep_w(w).start()
    for s in range(S):
        keep_in(2, s).start()
    read_all[z] = read_ref[...]
    for oz in range(1, Z):
        read_copy(oz, (z + Z - oz) % Z).wait_recv()
    for s in range(S):
        for kind in (1, 0):
            keep_in(kind, s).wait()
            give_in(kind, s, other).wait_recv()
        u_own[s] = state[s].astype(BF16)
    for _ in weight_steps(0):
        pass

    second = weight_steps(1)
    each(0, S, open_1)
    next(second, None)
    each(S, T, open_1)
    next(second, None)
    each(0, S, join_1)
    each(S, T, join_1)
    for _ in second:
        pass
    each(0, S, close_1)
    each(S, T, close_1)
    for s in range(S):
        give_in(2, s, a).start()
    each(0, T, join_2)
    each(0, T, close_2, 1.0)
    each(0, S, back_2)
    each(S, T, back_2)
    each(0, S, lambda s: exchange(0, [0, 1] + first_kinds, s))
    each(0, S, forward_1, True)
    each(S, T, forward_1, False)

    def step_end(s, step):
        moved = back_1(s, True)
        settle(s)
        fresh = state[s] - 0.005 * moved + 0.1 * noise[step, s]
        state[s] = fresh
        u_own[s] = fresh.astype(BF16)
        open_1(s)

    for s in range(S):
        keep_in(2, s).wait()
        give_in(2, s, other).wait_recv()
    each(0, S, step_end, 0)

    def data_end(s):
        back_1(S + s, False)
        settle(S + s)
        exchange(0, last_kinds, s)

    each(0, S, data_end)

    def langevin(step, carry):
        each(0, S, join_1)
        each(0, S, close_1)
        each(0, S, join_2)
        each(0, S, close_2, 1.0)
        each(0, S, back_2)
        each(0, S, forward_1, True)
        each(0, S, step_end, step)
        return carry

    lax.fori_loop(1, steps, langevin, 0)

    def contract(left, right):
        return lax.dot_general(
            left.reshape(-1, left.shape[-1]), right.reshape(-1, right.shape[-1]),
            (((0,), (0,)), ((), ())), preferred_element_type=F32,
        )

    each(0, S, lambda s: exchange(1, [0], s))
    each(0, S, join_1)
    each(0, S, close_1)
    each(0, S, lambda s: exchange(1, [1], s))
    each(0, S, join_2)
    arrived(0, range(2 + 2 * q))
    each(0, S, close_2, -1.0)
    for g, left, out_ref in ((1, rows_all, raw1_ref), (0, hid_all, raw2_ref)):
        for i in range(q):
            out_ref[:, i * C : (i + 1) * C] = contract(left[0], g_all[0, g, i])
    each(0, S, back_2)
    each(0, S, lambda s: exchange(1, first_kinds, s))
    each(0, S, forward_1, False)

    def last_end(s):
        back_1(s, False)
        exchange(1, last_kinds, s)

    each(0, S, last_end)

    squares = jnp.zeros((8, 128), F32)
    for g, left, out_ref in ((0, hid_all, raw2_ref), (1, rows_all, raw1_ref)):
        arrived(1, [1] + first_kinds if g == 0 else [0] + last_kinds)
        for i in range(q):
            at = slice(i * C, (i + 1) * C)
            raw = out_ref[:, at] + contract(left[1], g_all[1, g, i])
            out_ref[:, at] = raw
            squares += folded(raw * raw)
    own_stat[1] = squares
    gap = energy[S] - energy[0]
    for s in range(1, S):
        gap += energy[S + s] - energy[s]
    own_stat[0] = gap

    each(0, S, settle)
    for half in range(2):
        exchange_settle(half)
    for w in range(2):
        weight_settle(w)
    for oz in range(1, Z):
        read_copy(oz, z).wait_send()
    for kind in range(3):
        for s in range(S):
            give_in(kind, s, a).wait_send()

    base = 0
    for axis, count, peer in (("fsdp", X, x_peer), ("fsdp", Z, z_peer), ("dp", dpn, dp_peer)):
        copies = []
        for o in range(1, count):
            at = base + o - 1
            copy = send(own_stat, got_stat.at[at], sem_ts.at[at], sem_tr.at[at], {axis: peer(o)})
            copy.start()
            copies.append(copy)
        total = own_stat[...]
        for o, copy in enumerate(copies):
            copy.wait()
            total += got_stat[base + o]
        own_stat[...] = total
        base += count - 1
    stat_ref[...] = own_stat[...]


def solution(mesh):
    n, dpn = mesh.shape["fsdp"], mesh.shape["dp"]
    X = inner_of(n)
    Z = n // X
    K = Z // 2
    Y = dpn // 2
    q = n // dpn

    def local(data, start, noise, w1, w2, readout):
        R, C = start.shape
        H = w1.shape[1]
        steps = noise.shape[0]
        S = 2 if R % 64 == 0 else 1
        T = 2 * S
        h = R // T
        vmem = pl.BlockSpec(memory_space=pltpu.VMEM)
        hbm = pl.BlockSpec(memory_space=pl.ANY)
        dma = pltpu.SemaphoreType.DMA
        kinds = 2 + 2 * q
        others = 2 * dpn - 1
        peers = (X - 1) + (Z - 1) + (dpn - 1)
        wide = 2 * C
        X1, K1, Y1 = max(X - 1, 1), max(K - 1, 1), max(Y - 1, 1)
        raw1, raw2, stat = pl.pallas_call(
            functools.partial(kernel, n, X, dpn, steps, S),
            name="contrastive",
            out_shape=(
                jax.ShapeDtypeStruct((C, q * C), F32),
                jax.ShapeDtypeStruct((C, q * C), F32),
                jax.ShapeDtypeStruct((2, 8, 128), F32),
            ),
            in_specs=[hbm] * 5 + [vmem],
            out_specs=(vmem,) * 3,
            scratch_shapes=[
                pltpu.VMEM((wide, H), BF16),
                pltpu.VMEM((wide, H), BF16),
                pltpu.VMEM((S, h, wide), F32),
                pltpu.VMEM((steps, S, h, wide), F32),
                pltpu.VMEM((T, h, wide), BF16),
                pltpu.VMEM((T, h, wide), BF16),
                pltpu.VMEM((T, h, wide), F32),
                pltpu.VMEM((T, K, h, wide), F32),
                pltpu.VMEM((T, h, wide), F32),
                pltpu.VMEM((Z, 1, C), F32),
                pltpu.VMEM((T, 2, K, X1, h, wide), BF16),
                pltpu.VMEM((T, 2, K, X1, h, wide), BF16),
                pltpu.VMEM((T, 2 * K - 1, h, wide), BF16),
                pltpu.VMEM((T, K1, 1 + K, h, wide), BF16),
                pltpu.VMEM((T, 2, K * X, h, wide), BF16),
                pltpu.VMEM((2, 2 * dpn, S, h, C), BF16),
                pltpu.VMEM((2, 2 * dpn, S, h, C), BF16),
                pltpu.VMEM((2, 2, q, 2 * dpn, S, h, C), BF16),
                pltpu.VMEM((T, 8, 128), F32),
                pltpu.VMEM((2, 8, 128), F32),
                pltpu.VMEM((peers, 2, 8, 128), F32),
                dma((3 * S + 2,)),
                dma((3, S)), dma((3, S)),
                dma((Z - 1,)), dma((Z - 1,)),
                dma((2, PIECES)), dma((2, PIECES)),
                dma((2, PIECES, Y1)), dma((2, PIECES, Y1)),
                dma((2, PIECES, Y)), dma((2, PIECES, Y)),
                dma((T, 2, K, X1)), dma((T, 2, K, X1)),
                dma((T, K1, 1 + K)), dma((T, K1, 1 + K)),
                dma((T, K1)), dma((T, K1)),
                dma((T, 2, K, X1)), dma((T, 2, K, X1)),
                dma((2, kinds, others, S)), dma((2, kinds, others, S)),
                dma((peers,)), dma((peers,)),
            ],
            compiler_params=pltpu.CompilerParams(
                collective_id=0, has_side_effects=True, vmem_limit_bytes=60 * 1024 * 1024
            ),
        )(data, start, noise, w1, w2, readout.reshape(1, C))
        sums = jnp.sum(stat, axis=(1, 2))
        energy_gap = sums[0] / (R * dpn * 80.0 * jnp.sqrt(jnp.float32(H)))
        scale = jnp.sqrt(sums[1] / (2.0 * (C * n) * H) + 1e-06)
        return raw1 / scale, raw2 / scale, energy_gap

    in_specs = (
        P("dp", "fsdp"),
        P("dp", "fsdp"),
        P(None, "dp", "fsdp"),
        P("fsdp", None),
        P("fsdp", None),
        P("fsdp"),
    )
    out_specs = (P("fsdp", "dp"), P("fsdp", "dp"), P())
    return jax.shard_map(local, mesh=mesh, in_specs=in_specs, out_specs=out_specs, check_vma=False)
```

time: 377 us -> 357 us (0.947)
  Pallas kernels: 367 us -> 348 us
    pallas_call x1, Pallas kernels: 367 us -> 348 us  [local(): pl.pallas_call(functools.partial(kernel, n, X, dpn, steps, S), name='cont...]
where the time goes in v1:
time: 357 us
  Pallas kernels  348 us (97%)
  other arithmetic  5.86 us (2%)
    pallas_call x1, Pallas kernels, local(): pl.pallas_call(functools.partial(kernel, n, X, dpn, steps, S), name='cont...  348 us

profile of v1, /device:TPU:0, one launch (start us, length us, event | category | flops | bytes accessed | tf_op | source)
XLA Modules:
  0.0 357.1 jit_solution(14076492104477370625)
XLA Ops:
  0.6 347.5 %contrastive.1 = (f32[512,1024]{1,0:T(8,128)}, f32[512,1024]{1,0:T(8,128)}, f32[2,8,128]{2,1,0:T(8,128)}) custom-call(bf16[128,512]{1,0:T(8,128)(2,1)} %data_ref.1, f32[128,512]{1,0:T(8,128)} %start_ref.1, f32[4,128,512]{2,1,0:T(8,128)} %noise_in.1, bf16[512,4096]{1,0:T(8,128)(2,1)} %w1_ref.1, bf16[512,4096]{1,0:T(8,128)(2,1)} %w2_ref.1, f32[1,512]{1,0:T(1,128)} %bitcast.3), custom_call_target="tpu_custom_call" | custom-call | tf_op jit(solution)/shard_map/contrastive/pallas_call | solution.py:565
  348.1 0.8 reduce_sum.9
  348.9 0.6 fusion
  350.9 5.1 %broadcast_divide_fusion = (f32[512,1024]{1,0:T(8,128)}, f32[512,1024]{1,0:T(8,128)}) fusion(f32[512,1024]{1,0:T(8,128)} %get-tuple-element.8, f32[]{:T(128)} %bitcast.1, f32[512,1024]{1,0:T(8,128)} %get-tuple-element.6), kind=kLoop, calls=%fused_computation | loop fusion | flops 1048576 | bytes 8388612 | tf_op jit(solution)/shard_map/div | solution.py:617

commit v2 on v1

--- a/solution.py
+++ b/solution.py
@@ -30,9 +30,10 @@
     n, X, dpn, steps, S,
     data_ref, start_ref, noise_in, w1_ref, w2_ref, read_ref,
     raw1_ref, raw2_ref, stat_ref,
-    wm1, wm2, state, noise, u_own, hid, slope_1, acc, tot, read_all,
+    wm1, wm2, u_in, start_in, s_u, r_u, acc_u, s_v, r_v,
+    state, noise, u_own, hid, slope_1, acc, tot, read_all,
     s_a, r_a, s_b, r_b, buf, rows_all, hid_all, g_all, energy, own_stat, got_stat,
-    sem_l, sem_is, sem_ir, sem_rs, sem_rr, sem_wzs, sem_wzr, sem_wys, sem_wyr, sem_wcs, sem_wcr,
+    sem_l, sem_us, sem_ur, sem_vs, sem_vr, sem_is, sem_ir, sem_ns, sem_nr, sem_rs, sem_rr, sem_wzs, sem_wzr, sem_wys, sem_wyr, sem_wcs, sem_wcr,
     sem_as, sem_ar, sem_bs, sem_br, sem_zs, sem_zr, sem_xs, sem_xr, sem_ds, sem_dr, sem_ts, sem_tr,
 ):
     Z = n // X
@@ -102,20 +103,35 @@
     def rows_in(half, s):
         return pl.ds(pl.multiple_of((half * S + s) * h, h), h)
 
-    def pieces_in(kind, s, half, slot):
-        if kind == 0:
-            return data_ref.at[rows_in(half, s), :], u_own.at[S + s, :, half_cols(slot)]
-        if kind == 1:
-            return start_ref.at[rows_in(half, s), :], state.at[s, :, half_cols(slot)]
-        return noise_in.at[:, rows_in(half, s), :], noise.at[:, s, :, half_cols(slot)]
-
-    def keep_in(kind, s):
-        src, dst = pieces_in(kind, s, a, a)
-        return fetch(src, dst, sem_l.at[kind * S + s])
-
-    def give_in(kind, s, slot):
-        src, dst = pieces_in(kind, s, other, slot)
-        return send(src, dst, sem_is.at[kind, s], sem_ir.at[kind, s], partner)
+    def fetch_in(g, ad, s):
+        src, dst = ((start_ref, start_in.at[ad, s]), (data_ref, u_in.at[1, ad, s]))[g]
+        return fetch(src.at[rows_in(ad, s), :], dst, sem_l.at[2 + (g * 2 + ad) * S + s])
+
+    def give_state(s, slot):
+        return send(
+            start_in.at[other, s], state.at[s, :, half_cols(slot)], sem_is.at[s], sem_ir.at[s], partner
+        )
+
+    def keep_data(s):
+        return fetch(
+            data_ref.at[rows_in(a, s), :], u_own.at[S + s, :, half_cols(a)], sem_l.at[2 + 5 * S + s]
+        )
+
+    def give_data(s, slot):
+        return send(
+            u_in.at[1, other, s], u_own.at[S + s, :, half_cols(slot)], sem_is.at[S + s], sem_ir.at[S + s], partner
+        )
+
+    def keep_noise(s):
+        return fetch(
+            noise_in.at[:, rows_in(a, s), :], noise.at[:, s, :, half_cols(a)], sem_l.at[2 + 4 * S + s]
+        )
+
+    def give_noise(t, s, slot):
+        return send(
+            noise_in.at[t, rows_in(other, s), :], noise.at[t, s, :, half_cols(slot)],
+            sem_ns.at[t, s], sem_nr.at[t, s], partner,
+        )
 
     def read_copy(oz, at):
         return send(read_ref, read_all.at[at], sem_rs.at[oz - 1], sem_rr.at[oz - 1], {"fsdp": z_peer(oz)})
@@ -124,7 +140,7 @@
 
     def keep_w(w):
         src, dst = weights[w]
-        return fetch(src, dst.at[half_cols(a), :], sem_l.at[3 * S + w])
+        return fetch(src, dst.at[half_cols(a), :], sem_l.at[w])
 
     def w_rows(slot, d):
         return pl.ds(pl.multiple_of(slot * C + d * slice_rows, slice_rows), slice_rows)
@@ -168,7 +184,8 @@
         for p in range(PIECES):
             for o in range(Y):
                 wc_copy(w, p, o, y_source(o) * 2 + 1 - c).wait_recv()
-        keep_w(w).wait()
+        if w:
+            keep_w(1).wait()
 
     def weight_settle(w):
         for p in range(PIECES):
@@ -178,6 +195,71 @@
             for o in range(Y):
                 wc_copy(w, p, o, dpi).wait_send()
 
+    order = list(range(1, K)) + [0]
+
+    def ua_copy(g, ok, ox):
+        return send(
+            s_u.at[g, ok, ox - 1], r_u.at[g, ok, ox - 1], sem_us.at[g, ok, ox - 1], sem_ur.at[g, ok, ox - 1],
+            {"fsdp": x_peer(ox)},
+        )
+
+    def ub_copy(g, ok, oa):
+        ad = (a + oa) % 2
+        return send(
+            s_v.at[g, ok, ad], r_v.at[g, ok, oa], sem_vs.at[g, ok, oa], sem_vr.at[g, ok, oa],
+            {"fsdp": device((k + ok) % K, ad, x)},
+        )
+
+    def first_open(g):
+        lhs = u_in[g].reshape(T * h, C)
+        for own in range(2):
+            for ok in order:
+                for ox in [0] if own else range(1, X):
+                    for i in range(2):
+                        cols = shard_cols((k + ok) % K, i, (x + ox) % X)
+                        part = jnp.dot(lhs, wm1[half_cols(a), cols], preferred_element_type=F32)
+                        if own:
+                            acc_u[g, ok, :, i * C : (i + 1) * C] = part
+                        else:
+                            s_u[g, ok, ox - 1, :, i * C : (i + 1) * C] = part.astype(BF16)
+                    if not own:
+                        ua_copy(g, ok, ox).start()
+
+    def first_join(g, ok):
+        total = acc_u[g, ok]
+        for ox in range(1, X):
+            ua_copy(g, ok, ox).wait_recv()
+            total += r_u[g, ok, ox - 1].astype(F32)
+        s_v[g, ok] = total.astype(BF16).reshape(2, S * h, 2 * C)
+        for oa in (0, 1):
+            if ok or oa:
+                ub_copy(g, ok, oa).start()
+        if ok == 0:
+            acc_u[g, 0] = total
+
+    def first_close(g):
+        a1 = acc_u[g, 0, pl.ds(pl.multiple_of(a * S * h, S * h), S * h), :]
+        for ok in order:
+            for oa in (0, 1):
+                if ok or oa:
+                    ub_copy(g, ok, oa).wait_recv()
+                    a1 += r_v[g, ok, oa].astype(F32)
+        s1 = jax.nn.sigmoid(a1)
+        hidden = (a1 * s1).astype(BF16)
+        slope = s1 * (1.0 + a1 * (1.0 - s1))
+        for s in range(S):
+            hid[g * S + s] = hidden[s * h : (s + 1) * h]
+            slope_1[g * S + s] = slope[s * h : (s + 1) * h]
+
+    def first_settle():
+        for g in range(1):
+            for ok in range(K):
+                for ox in range(1, X):
+                    ua_copy(g, ok, ox).wait_send()
+                for oa in (0, 1):
+                    if ok or oa:
+                        ub_copy(g, ok, oa).wait_send()
+
     def a_copy(s, j, ok, ox):
         return send(
             s_a.at[s, j, ok, ox - 1], r_a.at[s, j, ok, ox - 1],
@@ -190,8 +272,6 @@
             s_b.at[s, ok - 1 if j == 0 else K - 1 + part], r_b.at[s, ok - 1, at],
             sem_bs.at[s, ok - 1, at], sem_br.at[s, ok - 1, at], {"fsdp": k_peer(ok)},
         )
-
-    order = list(range(1, K)) + [0]
 
     def two_dots(lhs, w, kd, xd):
         return [
@@ -204,9 +284,40 @@
                 for i, part in enumerate(two_dots(lhs, w, (k + ok) % K, (x + ox) % X)):
                     s_a[s, j, ok, ox - 1, :, i * C : (i + 1) * C] = part.astype(BF16)
                 a_copy(s, j, ok, ox).start()
+
+    def pair(ref, low):
+        return ref[pl.ds(low, S)].reshape(S * h, 2 * C)
+
+    def pair_open(low, j, lhs, w):
+        for ok in order:
+            for ox in range(1, X):
+                for i, part in enumerate(two_dots(lhs, w, (k + ok) % K, (x + ox) % X)):
+                    for s in range(S):
+                        s_a[low + s, j, ok, ox - 1, :, i * C : (i + 1) * C] = part[s * h : (s + 1) * h].astype(BF16)
+                for s in range(S):
+                    a_copy(low + s, j, ok, ox).start()
+
+    def pair_own(low, lhs, w):
         for ok in order:
             for i, part in enumerate(two_dots(lhs, w, (k + ok) % K, x)):
-                acc[s, ok, :, i * C : (i + 1) * C] = part
+                for s in range(S):
+                    acc[low + s, ok, :, i * C : (i + 1) * C] = part[s * h : (s + 1) * h]
+
+    def own_1(low):
+        pair_own(low, pair(u_own, low), wm1)
+
+    def own_2(low):
+        pair_own(low, pair(hid, low), wm2)
+
+    def pair_block(low, stage, kd, xd, w):
+        total = None
+        for i in range(2):
+            lhs = buf[pl.ds(low, S), stage, kd * X + xd, :, i * C : (i + 1) * C].reshape(S * h, C)
+            part = lax.dot_general(
+                lhs, w[:, shard_cols(kd, i, xd)], (((1,), (1,)), ((), ())), preferred_element_type=F32
+            )
+            total = part if total is None else total + part
+        return total
 
     def joined(s, j, ok):
         total = acc[s, ok]
@@ -223,7 +334,7 @@
             s_b[s, ok - 1] = joined(s, 0, ok).astype(BF16)
             b_copy(s, 0, ok, 0).start()
 
-    def close_1(s):
+    def hidden_1(s):
         a1 = joined(s, 0, 0)
         for ok in range(1, K):
             b_copy(s, 0, ok, 0).wait_recv()
@@ -231,6 +342,9 @@
         s1 = jax.nn.sigmoid(a1)
         hid[s] = (a1 * s1).astype(BF16)
         slope_1[s] = s1 * (1.0 + a1 * (1.0 - s1))
+
+    def close_1(s):
+        hidden_1(s)
         scatter_open(s, 1, hid[s], wm2)
 
     def join_2(s):
@@ -276,11 +390,13 @@
                 x_copy(s, 0, ok, ox, kd * X + x).start()
             if ok == 0:
                 energy[s] = folded(gain * (a2 * s2))
+
+    def mid_2(low):
         total = None
         for ok in order:
-            part = block(s, 0, (k + ok) % K, x, wm2)
+            part = pair_block(low, 0, (k + ok) % K, x, wm2)
             total = part if total is None else total + part
-        tot[s] = total
+        tot[pl.ds(low, S)] = total.reshape(S, h, 2 * C)
 
     def back_2(s):
         total = tot[s]
@@ -289,29 +405,51 @@
                 kd, xd = (k + ok) % K, (x + X - ox) % X
                 x_copy(s, 0, ok, ox, kd * X + xd).wait_recv()
                 total += block(s, 0, kd, xd, wm2)
+        give_1(s, total)
+
+    def give_1(s, total):
         buf[s, 1, self_at] = (total * slope_1[s]).astype(BF16)
         for ok in range(1, K):
             z_copy(s, ok, self_at).start()
         for ox in range(1, X):
             x_copy(s, 1, 0, ox, self_at).start()
 
-    def forward_1(s, moving):
-        if moving:
-            total = block(s, 1, k, x, wm1)
+    def pair_back_2(low):
+        total = tot[pl.ds(low, S)].reshape(S * h, 2 * C)
+        for ok in order:
+            for ox in range(1, X):
+                kd, xd = (k + ok) % K, (x + X - ox) % X
+                for s in range(S):
+                    x_copy(low + s, 0, ok, ox, kd * X + xd).wait_recv()
+                total += pair_block(low, 0, kd, xd, wm2)
+        for s in range(S):
+            give_1(low + s, total[s * h : (s + 1) * h])
+
+    def mid_1():
+        tot[0:S] = pair_block(0, 1, k, x, wm1).reshape(S, h, 2 * C)
+
+    def forward_1(s):
         for ok in range(1, K):
             kd = (k + K - ok) % K
             z_copy(s, ok, kd * X + x).wait_recv()
             for ox in range(1, X):
                 x_copy(s, 1, ok, ox, kd * X + x).start()
-            if moving:
-                total += block(s, 1, kd, x, wm1)
-        if moving:
-            tot[s] = total
+
+    def more_1():
+        total = tot[0:S].reshape(S * h, 2 * C)
+        for ok in range(1, K):
+            total += pair_block(0, 1, (k + K - ok) % K, x, wm1)
+        for ox in range(1, X):
+            xd = (x + X - ox) % X
+            for s in range(S):
+                x_copy(s, 1, 0, ox, k * X + xd).wait_recv()
+            total += pair_block(0, 1, k, xd, wm1)
+        tot[0:S] = total.reshape(S, h, 2 * C)
 
     def back_1(s, moving):
         if moving:
             total = tot[s]
-        for ok in range(K):
+        for ok in range(1, K) if moving else range(K):
             for ox in range(1, X):
                 kd, xd = (k + K - ok) % K, (x + X - ox) % X
                 x_copy(s, 1, ok, ox, kd * X + xd).wait_recv()
@@ -320,24 +458,26 @@
         if moving:
             return total
 
-    def settle(s):
+    def settle(s, first=False):
         for j in range(2):
             for ok in range(K):
                 for ox in range(1, X):
-                    a_copy(s, j, ok, ox).wait_send()
+                    if j or not first:
+                        a_copy(s, j, ok, ox).wait_send()
                     x_copy(s, j, ok, ox, self_at).wait_send()
         for ok in range(1, K):
-            b_copy(s, 0, ok, 0).wait_send()
+            if not first:
+                b_copy(s, 0, ok, 0).wait_send()
             for part in range(K):
                 b_copy(s, 1, ok, part).wait_send()
             z_copy(s, ok, self_at).wait_send()
 
-    def place(half, kind, p, s):
+    def place(half, kind, d, ad, s):
         if kind == 0:
-            return rows_all.at[half, p, s]
+            return rows_all.at[half, d, ad, s]
         if kind == 1:
-            return hid_all.at[half, p, s]
-        return g_all.at[half, (kind - 2) // q, (kind - 2) % q, p, s]
+            return hid_all.at[half, d, ad, s]
+        return g_all.at[half, (kind - 2) // q, (kind - 2) % q, d, ad, s]
 
     def source(half, kind, s, ad, dd):
         at = s if half else S + s
@@ -350,36 +490,47 @@
         zd, xd = shard // X, shard % X
         return buf.at[at, stage, (zd // 2) * X + xd, :, half_cols(zd % 2)]
 
-    mine = a * dpn + dpi
-
-    def swap(half, kind, e, s, p):
+    def swap(half, kind, e, s, d, ad):
         oa, od = offsets[e]
         return send(
-            source(half, kind, s, (a + oa) % 2, dp_peer(od)), place(half, kind, p, s),
+            source(half, kind, s, (a + oa) % 2, dp_peer(od)), place(half, kind, d, ad, s),
             sem_ds.at[half, kind, e, s], sem_dr.at[half, kind, e, s], swap_peer(oa, od),
         )
 
-    def exchange(half, kinds, s):
+    def rows_copy(o, d):
+        return send(
+            u_in.at[1], rows_all.at[0, d], sem_ds.at[0, 0, o - 1, 0], sem_dr.at[0, 0, o - 1, 0], {"dp": dp_peer(o)}
+        )
+
+    def exchange_part(half, kinds, s, part):
         for kind in kinds:
-            for e in range(len(offsets)):
-                swap(half, kind, e, s, mine).start()
+            for e, (oa, _) in enumerate(offsets):
+                if oa == part:
+                    swap(half, kind, e, s, dpi, a).start()
+
+    def exchange_near(half, kinds, s):
+        exchange_part(half, kinds, s, 0)
         for kind in kinds:
-            place(half, kind, mine, s)[...] = source(half, kind, s, a, dpi)[...]
+            place(half, kind, dpi, a, s)[...] = source(half, kind, s, a, dpi)[...]
+
+    def exchange_far(half, kinds, s):
+        exchange_part(half, kinds, s, 1)
 
     def arrived(half, kinds):
         def one(s):
             for kind in kinds:
                 for e, (oa, od) in enumerate(offsets):
-                    p = ((a + oa) % 2) * dpn + (dpi + dpn - od) % dpn
-                    swap(half, kind, e, s, p).wait_recv()
+                    swap(half, kind, e, s, (dpi + dpn - od) % dpn, (a + oa) % 2).wait_recv()
 
         each(0, S, one)
+
+    data_kinds = range(1, 2 + 2 * q)
 
     def exchange_settle(half):
         def one(s):
-            for kind in range(2 + 2 * q):
+            for kind in range(2 + 2 * q) if half else data_kinds:
                 for e in range(len(offsets)):
-                    swap(half, kind, e, s, mine).wait_send()
+                    swap(half, kind, e, s, dpi, a).wait_send()
 
         each(0, S, one)
 
@@ -392,84 +543,174 @@
 
     first_kinds, last_kinds = [2 + i for i in range(q)], [2 + q + i for i in range(q)]
 
-    for s in range(S):
-        give_in(1, s, a).start()
-        give_in(0, s, a).start()
-    for w in range(2):
-        for p in range(PIECES):
-            wz_copy(w, p, a).start()
+    for p in range(PIECES):
+        wz_copy(1, p, a).start()
+    for s in range(S):
+        for ad in range(2):
+            fetch_in(0, ad, s).start()
+    keep_w(0).start()
+    for s in range(S):
+        for ad in range(2):
+            fetch_in(1, ad, s).start()
+    keep_w(1).start()
+    for s in range(S):
+        keep_data(s).start()
+        keep_noise(s).start()
     for oz in range(1, Z):
         read_copy(oz, z).start()
     for s in range(S):
-        keep_in(1, s).start()
-        keep_in(0, s).start()
-    for w in range(2):
-        keep_w(w).start()
-    for s in range(S):
-        keep_in(2, s).start()
+        for ad in range(2):
+            fetch_in(0, ad, s).wait()
+    u_in[0] = start_in[...].astype(BF16)
+    keep_w(0).wait()
+    first_open(0)
     read_all[z] = read_ref[...]
-    for oz in range(1, Z):
-        read_copy(oz, (z + Z - oz) % Z).wait_recv()
-    for s in range(S):
-        for kind in (1, 0):
-            keep_in(kind, s).wait()
-            give_in(kind, s, other).wait_recv()
-        u_own[s] = state[s].astype(BF16)
-    for _ in weight_steps(0):
-        pass
-
-    second = weight_steps(1)
-    each(0, S, open_1)
-    next(second, None)
-    each(S, T, open_1)
-    next(second, None)
-    each(0, S, join_1)
-    each(S, T, join_1)
-    for _ in second:
-        pass
-    each(0, S, close_1)
-    each(S, T, close_1)
-    for s in range(S):
-        give_in(2, s, a).start()
-    each(0, T, join_2)
-    each(0, T, close_2, 1.0)
-    each(0, S, back_2)
-    each(S, T, back_2)
-    each(0, S, lambda s: exchange(0, [0, 1] + first_kinds, s))
-    each(0, S, forward_1, True)
-    each(S, T, forward_1, False)
-
-    def step_end(s, step):
+    for s in range(S):
+        state[s, :, half_cols(a)] = start_in[a, s]
+    def step_end(s, step, first=False):
         moved = back_1(s, True)
-        settle(s)
+        settle(s, first)
+        give_noise(step, s, other).wait_recv()
         fresh = state[s] - 0.005 * moved + 0.1 * noise[step, s]
         state[s] = fresh
         u_own[s] = fresh.astype(BF16)
         open_1(s)
 
     for s in range(S):
-        keep_in(2, s).wait()
-        give_in(2, s, other).wait_recv()
-    each(0, S, step_end, 0)
-
-    def data_end(s):
-        back_1(S + s, False)
-        settle(S + s)
-        exchange(0, last_kinds, s)
-
-    each(0, S, data_end)
+        for ad in range(2):
+            fetch_in(1, ad, s).wait()
+    second, first = weight_steps(1), weight_steps(0)
+    for ok in order:
+        next(second)
+        first_join(0, ok)
+    for p in range(PIECES // 2):
+        wz_copy(0, p, a).start()
+    for _ in second:
+        pass
+    for oz in range(1, Z):
+        read_copy(oz, (z + Z - oz) % Z).wait_recv()
+    first_close(0)
+    pair_open(0, 1, pair(hid, 0), wm2)
+    own_2(0)
+    next(first)
+    each(0, S, join_2)
+    for p in range(PIECES // 2, PIECES):
+        wz_copy(0, p, a).start()
+    for s in range(S):
+        give_state(s, a).start()
+        give_noise(0, s, a).start()
+    next(first)
+    each(0, S, close_2, 1.0)
+    mid_2(0)
+    next(first)
+    each(0, S, back_2)
+    for s in range(S):
+        give_data(s, a).start()
+    for _ in first:
+        pass
+    mid_1()
+    each(0, S, forward_1)
+    more_1()
+    if steps > 1:
+        for s in range(S):
+            give_noise(1, s, a).start()
+    for o in range(1, dpn):
+        rows_copy(o, dpi).start()
+    rows_all[0, dpi] = u_in[1]
+
+    for s in range(S):
+        keep_noise(s).wait()
+        give_state(s, other).wait_recv()
+    each(0, S, step_end, 0, True)
+    own_1(0)
+
+    def swap_task(kind, s):
+        def task():
+            exchange_near(0, [kind], s)
+            exchange_far(0, [kind], s)
+
+        return task
+
+    def data_open():
+        for s in range(S):
+            keep_data(s).wait()
+            give_data(s, other).wait_recv()
+        pair_open(S, 0, pair(u_own, S), wm1)
+        own_1(S)
+
+    def data_middle():
+        each(S, T, hidden_1)
+        pair_open(S, 1, pair(hid, S), wm2)
+        own_2(S)
+
+    def data_close():
+        each(S, T, close_2, 1.0)
+
+    def data_back():
+        mid_2(S)
+        pair_back_2(S)
+
+    def data_last():
+        def last(s):
+            back_1(s, False)
+            settle(s)
+
+        each(S, T, last)
+
+    heavy = [
+        data_open, lambda: each(S, T, join_1), data_middle, lambda: each(S, T, join_2), data_close,
+        data_back, lambda: each(S, T, forward_1), data_last,
+    ]
+    light = [[] for _ in range(4 * max(steps - 1, 0))]
+    late = []
+    ready = {3: [1], 6: first_kinds, 8: last_kinds}
+    at = 0
+    for begin, kinds in ready.items():
+        at = max(at, begin)
+        for kind in kinds:
+            for s in range(S):
+                (light[at] if at < len(light) else late).append(swap_task(kind, s))
+                at += s % 2 if kind > 1 + q else 1
+
+    def slot(step, i):
+        for t in range(1, steps):
+            at = (t - 1) * 4 + i
+            tasks = heavy[at : at + 1] + light[at]
+            if tasks:
+
+                @pl.when(step == t)
+                def _(tasks=tasks):
+                    for task in tasks:
+                        task()
 
     def langevin(step, carry):
         each(0, S, join_1)
+        slot(step, 0)
         each(0, S, close_1)
+        own_2(0)
         each(0, S, join_2)
+        slot(step, 1)
         each(0, S, close_2, 1.0)
+        mid_2(0)
         each(0, S, back_2)
-        each(0, S, forward_1, True)
+        slot(step, 2)
+        mid_1()
+        each(0, S, forward_1)
+        more_1()
+
+        @pl.when(step + 1 < steps)
+        def _():
+            for s in range(S):
+                give_noise(step + 1, s, a).start()
+
+        slot(step, 3)
         each(0, S, step_end, step)
+        own_1(0)
         return carry
 
     lax.fori_loop(1, steps, langevin, 0)
+    for task in heavy[4 * max(steps - 1, 0) :] + late:
+        task()
 
     def contract(left, right):
         return lax.dot_general(
@@ -477,25 +718,34 @@
             (((0,), (0,)), ((), ())), preferred_element_type=F32,
         )
 
-    each(0, S, lambda s: exchange(1, [0], s))
+    for part in (exchange_near, exchange_far):
+        each(0, S, lambda s: part(1, [0], s))
     each(0, S, join_1)
     each(0, S, close_1)
-    each(0, S, lambda s: exchange(1, [1], s))
+    own_2(0)
+    for part in (exchange_near, exchange_far):
+        each(0, S, lambda s: part(1, [1], s))
     each(0, S, join_2)
-    arrived(0, range(2 + 2 * q))
     each(0, S, close_2, -1.0)
+    mid_2(0)
+    each(0, S, back_2)
+    each(0, S, lambda s: exchange_near(1, first_kinds, s))
+    each(0, S, forward_1)
+    each(0, S, lambda s: exchange_far(1, first_kinds, s))
+
+    def last_end(s):
+        back_1(s, False)
+        exchange_near(1, last_kinds, s)
+        exchange_far(1, last_kinds, s)
+
+    each(0, S, last_end)
+
+    for o in range(1, dpn):
+        rows_copy(o, (dpi + dpn - o) % dpn).wait_recv()
+    arrived(0, data_kinds)
     for g, left, out_ref in ((1, rows_all, raw1_ref), (0, hid_all, raw2_ref)):
         for i in range(q):
             out_ref[:, i * C : (i + 1) * C] = contract(left[0], g_all[0, g, i])
-    each(0, S, back_2)
-    each(0, S, lambda s: exchange(1, first_kinds, s))
-    each(0, S, forward_1, False)
-
-    def last_end(s):
-        back_1(s, False)
-        exchange(1, last_kinds, s)
-
-    each(0, S, last_end)
 
     squares = jnp.zeros((8, 128), F32)
     for g, left, out_ref in ((0, hid_all, raw2_ref), (1, rows_all, raw1_ref)):
@@ -518,9 +768,14 @@
         weight_settle(w)
     for oz in range(1, Z):
         read_copy(oz, z).wait_send()
-    for kind in range(3):
-        for s in range(S):
-            give_in(kind, s, a).wait_send()
+    for s in range(S):
+        give_state(s, a).wait_send()
+        give_data(s, a).wait_send()
+        for t in range(steps):
+            give_noise(t, s, a).wait_send()
+    for o in range(1, dpn):
+        rows_copy(o, dpi).wait_send()
+    first_settle()
 
     base = 0
     for axis, count, peer in (("fsdp", X, x_peer), ("fsdp", Z, z_peer), ("dp", dpn, dp_peer)):
@@ -575,6 +830,13 @@
             scratch_shapes=[
                 pltpu.VMEM((wide, H), BF16),
                 pltpu.VMEM((wide, H), BF16),
+                pltpu.VMEM((2, 2, S, h, C), BF16),
+                pltpu.VMEM((2, S, h, C), F32),
+                pltpu.VMEM((1, K, X1, R, wide), BF16),
+                pltpu.VMEM((1, K, X1, R, wide), BF16),
+                pltpu.VMEM((1, K, R, wide), F32),
+                pltpu.VMEM((1, K, 2, S * h, wide), BF16),
+                pltpu.VMEM((1, K, 2, S * h, wide), BF16),
                 pltpu.VMEM((S, h, wide), F32),
                 pltpu.VMEM((steps, S, h, wide), F32),
                 pltpu.VMEM((T, h, wide), BF16),
@@ -588,14 +850,17 @@
                 pltpu.VMEM((T, 2 * K - 1, h, wide), BF16),
                 pltpu.VMEM((T, K1, 1 + K, h, wide), BF16),
                 pltpu.VMEM((T, 2, K * X, h, wide), BF16),
-                pltpu.VMEM((2, 2 * dpn, S, h, C), BF16),
-                pltpu.VMEM((2, 2 * dpn, S, h, C), BF16),
-                pltpu.VMEM((2, 2, q, 2 * dpn, S, h, C), BF16),
+                pltpu.VMEM((2, dpn, 2, S, h, C), BF16),
+                pltpu.VMEM((2, dpn, 2, S, h, C), BF16),
+                pltpu.VMEM((2, 2, q, dpn, 2, S, h, C), BF16),
                 pltpu.VMEM((T, 8, 128), F32),
                 pltpu.VMEM((2, 8, 128), F32),
                 pltpu.VMEM((peers, 2, 8, 128), F32),
-                dma((3 * S + 2,)),
-                dma((3, S)), dma((3, S)),
+                dma((2 + 6 * S,)),
+                dma((1, K, X1)), dma((1, K, X1)),
+                dma((1, K, 2)), dma((1, K, 2)),
+                dma((T,)), dma((T,)),
+                dma((steps, S)), dma((steps, S)),
                 dma((Z - 1,)), dma((Z - 1,)),
                 dma((2, PIECES)), dma((2, PIECES)),
                 dma((2, PIECES, Y1)), dma((2, PIECES, Y1)),

time: 357 us -> 285 us (0.80)
  Pallas kernels: 348 us -> 276 us
    pallas_call x1, Pallas kernels: 348 us -> 276 us  [local(): pl.pallas_call(functools.partial(kernel, n, X, dpn, steps, S), name='cont...]
where the time goes in v2:
time: 285 us
  Pallas kernels  276 us (97%)
  other arithmetic  5.86 us (2%)
  between operations  3.11 us (1%)
    pallas_call x1, Pallas kernels, local(): pl.pallas_call(functools.partial(kernel, n, X, dpn, steps, S), name='cont...  276 us

profile of v2, /device:TPU:0, one launch (start us, length us, event | category | flops | bytes accessed | tf_op | source)
XLA Modules:
  0.0 285.2 jit_solution(13337743642566295785)
XLA Ops:
  0.6 275.6 %contrastive.1 = (f32[512,1024]{1,0:T(8,128)}, f32[512,1024]{1,0:T(8,128)}, f32[2,8,128]{2,1,0:T(8,128)}) custom-call(bf16[128,512]{1,0:T(8,128)(2,1)} %data_ref.1, f32[128,512]{1,0:T(8,128)} %start_ref.1, f32[4,128,512]{2,1,0:T(8,128)} %noise_in.1, bf16[512,4096]{1,0:T(8,128)(2,1)} %w1_ref.1, bf16[512,4096]{1,0:T(8,128)(2,1)} %w2_ref.1, f32[1,512]{1,0:T(1,128)} %bitcast.3), custom_call_target="tpu_custom_call" | custom-call | tf_op jit(solution)/shard_map/contrastive/pallas_call | solution.py:820
  276.2 0.8 reduce_sum.9
  277.0 0.6 fusion
  279.0 5.1 %broadcast_divide_fusion = (f32[512,1024]{1,0:T(8,128)}, f32[512,1024]{1,0:T(8,128)}) fusion(f32[512,1024]{1,0:T(8,128)} %get-tuple-element.8, f32[]{:T(128)} %bitcast.1, f32[512,1024]{1,0:T(8,128)} %get-tuple-element.6), kind=kLoop, calls=%fused_computation | loop fusion | flops 1048576 | bytes 8388612 | tf_op jit(solution)/shard_map/div | solution.py:882

commit v3 on v2

--- a/solution.py
+++ b/solution.py
@@ -10,7 +10,9 @@
 MESH = pl.DeviceIdType.MESH
 BF16 = jnp.bfloat16
 F32 = jnp.float32
-PIECES = 4
+PIECES = 8
+EARLY = 2
+TASK_SLOTS = (0, 1, 2, 3, 4, 5, 6, 7)
 
 
 def inner_of(n):
@@ -29,7 +31,7 @@
 def kernel(
     n, X, dpn, steps, S,
     data_ref, start_ref, noise_in, w1_ref, w2_ref, read_ref,
-    raw1_ref, raw2_ref, stat_ref,
+    raw1_out, raw2_out, stat_ref, raw1_ref, raw2_ref,
     wm1, wm2, u_in, start_in, s_u, r_u, acc_u, s_v, r_v,
     state, noise, u_own, hid, slope_1, acc, tot, read_all,
     s_a, r_a, s_b, r_b, buf, rows_all, hid_all, g_all, energy, own_stat, got_stat,
@@ -186,6 +188,10 @@
                 wc_copy(w, p, o, y_source(o) * 2 + 1 - c).wait_recv()
         if w:
             keep_w(1).wait()
+
+    def advance(steps_of):
+        for _ in range(PIECES // 4):
+            next(steps_of)
 
     def weight_settle(w):
         for p in range(PIECES):
@@ -581,9 +587,9 @@
             fetch_in(1, ad, s).wait()
     second, first = weight_steps(1), weight_steps(0)
     for ok in order:
-        next(second)
+        advance(second)
         first_join(0, ok)
-    for p in range(PIECES // 2):
+    for p in range(PIECES * EARLY // 4):
         wz_copy(0, p, a).start()
     for _ in second:
         pass
@@ -592,17 +598,17 @@
     first_close(0)
     pair_open(0, 1, pair(hid, 0), wm2)
     own_2(0)
-    next(first)
+    advance(first)
     each(0, S, join_2)
-    for p in range(PIECES // 2, PIECES):
+    for p in range(PIECES * EARLY // 4, PIECES):
         wz_copy(0, p, a).start()
     for s in range(S):
         give_state(s, a).start()
         give_noise(0, s, a).start()
-    next(first)
+    advance(first)
     each(0, S, close_2, 1.0)
     mid_2(0)
-    next(first)
+    advance(first)
     each(0, S, back_2)
     for s in range(S):
         give_data(s, a).start()
@@ -661,9 +667,11 @@
         data_open, lambda: each(S, T, join_1), data_middle, lambda: each(S, T, join_2), data_close,
         data_back, lambda: each(S, T, forward_1), data_last,
     ]
-    light = [[] for _ in range(4 * max(steps - 1, 0))]
+    places = 4 * max(steps - 1, 0)
+    duty = {at: task for at, task in zip(TASK_SLOTS, heavy)}
+    light = [[] for _ in range(places)]
     late = []
-    ready = {3: [1], 6: first_kinds, 8: last_kinds}
+    ready = {TASK_SLOTS[2] + 1: [1], TASK_SLOTS[5] + 1: first_kinds, TASK_SLOTS[7] + 1: last_kinds}
     at = 0
     for begin, kinds in ready.items():
         at = max(at, begin)
@@ -675,7 +683,7 @@
     def slot(step, i):
         for t in range(1, steps):
             at = (t - 1) * 4 + i
-            tasks = heavy[at : at + 1] + light[at]
+            tasks = ([duty[at]] if at in duty else []) + light[at]
             if tasks:
 
                 @pl.when(step == t)
@@ -709,7 +717,7 @@
         return carry
 
     lax.fori_loop(1, steps, langevin, 0)
-    for task in heavy[4 * max(steps - 1, 0) :] + late:
+    for task in [duty[at] for at in TASK_SLOTS if at >= places] + late:
         task()
 
     def contract(left, right):
@@ -747,6 +755,10 @@
         for i in range(q):
             out_ref[:, i * C : (i + 1) * C] = contract(left[0], g_all[0, g, i])
 
+    def leave(g):
+        src, dst = ((raw2_ref, raw2_out), (raw1_ref, raw1_out))[g]
+        return fetch(src, dst, sem_l.at[g])
+
     squares = jnp.zeros((8, 128), F32)
     for g, left, out_ref in ((0, hid_all, raw2_ref), (1, rows_all, raw1_ref)):
         arrived(1, [1] + first_kinds if g == 0 else [0] + last_kinds)
@@ -755,6 +767,7 @@
             raw = out_ref[:, at] + contract(left[1], g_all[1, g, i])
             out_ref[:, at] = raw
             squares += folded(raw * raw)
+        leave(g).start()
     own_stat[1] = squares
     gap = energy[S] - energy[0]
     for s in range(1, S):
@@ -791,7 +804,13 @@
             total += got_stat[base + o]
         own_stat[...] = total
         base += count - 1
-    stat_ref[...] = own_stat[...]
+    total = own_stat[...]
+    gap = jnp.sum(total[0], axis=(0, 1), keepdims=True)
+    mean = jnp.sum(total[1], axis=(0, 1), keepdims=True) / (2.0 * (C * n) * H)
+    stat_ref[0] = jnp.broadcast_to(gap, (8, 128))
+    stat_ref[1] = jnp.broadcast_to(1.0 / jnp.sqrt(mean + 1e-06), (8, 128))
+    for g in range(2):
+        leave(g).wait()
 
 
 def solution(mesh):
@@ -826,8 +845,10 @@
                 jax.ShapeDtypeStruct((2, 8, 128), F32),
             ),
             in_specs=[hbm] * 5 + [vmem],
-            out_specs=(vmem,) * 3,
+            out_specs=(hbm, hbm, vmem),
             scratch_shapes=[
+                pltpu.VMEM((C, q * C), F32),
+                pltpu.VMEM((C, q * C), F32),
                 pltpu.VMEM((wide, H), BF16),
                 pltpu.VMEM((wide, H), BF16),
                 pltpu.VMEM((2, 2, S, h, C), BF16),
@@ -876,10 +897,8 @@
                 collective_id=0, has_side_effects=True, vmem_limit_bytes=60 * 1024 * 1024
             ),
         )(data, start, noise, w1, w2, readout.reshape(1, C))
-        sums = jnp.sum(stat, axis=(1, 2))
-        energy_gap = sums[0] / (R * dpn * 80.0 * jnp.sqrt(jnp.float32(H)))
-        scale = jnp.sqrt(sums[1] / (2.0 * (C * n) * H) + 1e-06)
-        return raw1 / scale, raw2 / scale, energy_gap
+        energy_gap = stat[0, 0, 0] / (R * dpn * 80.0 * jnp.sqrt(jnp.float32(H)))
+        return raw1 * stat[1, 0, 0], raw2 * stat[1, 0, 0], energy_gap
 
     in_specs = (
         P("dp", "fsdp"),

time: 285 us -> 281 us (0.986)
  Pallas kernels: 276 us -> 271 us
    mul x0 -> x1, other arithmetic: none -> 5.62 us  [local(): return (raw1 * stat[1, 0, 0], raw2 * stat[1, 0, 0], energy_gap)]
    div x1 -> x0, other arithmetic: 5.07 us -> none  [local(): return (raw1 / scale, raw2 / scale, energy_gap)]
    pallas_call x1, Pallas kernels: 276 us -> 271 us  [local(): pl.pallas_call(functools.partial(kernel, n, X, dpn, steps, S), name='cont...]
where the time goes in v3:
time: 281 us; the launch traced here: 280 us
  Pallas kernels  271 us (96%)
  other arithmetic  5.62 us (2%)
    pallas_call x1, Pallas kernels, local(): pl.pallas_call(functools.partial(kernel, n, X, dpn, steps, S), name='cont...  271 us
    mul x1, other arithmetic, local(): return (raw1 * stat[1, 0, 0], raw2 * stat[1, 0, 0], energy_gap)  5.62 us

profile of v3, /device:TPU:0, one launch (start us, length us, event | category | flops | bytes accessed | tf_op | source)
XLA Modules:
  0.0 280.3 jit_solution(5578446735818489217)
XLA Ops:
  0.6 271.1 %contrastive.1 = (f32[512,1024]{1,0:T(8,128)}, f32[512,1024]{1,0:T(8,128)}, f32[2,8,128]{2,1,0:T(8,128)}) custom-call(bf16[128,512]{1,0:T(8,128)(2,1)} %data_ref.1, f32[128,512]{1,0:T(8,128)} %start_ref.1, f32[4,128,512]{2,1,0:T(8,128)} %noise_in.1, bf16[512,4096]{1,0:T(8,128)(2,1)} %w1_ref.1, bf16[512,4096]{1,0:T(8,128)(2,1)} %w2_ref.1, f32[1,512]{1,0:T(1,128)} %bitcast.3), custom_call_target="tpu_custom_call" | custom-call | tf_op jit(solution)/shard_map/contrastive/pallas_call | solution.py:839
  271.7 1.2 fusion
  273.6 5.6 %broadcast_multiply_fusion = (f32[512,1024]{1,0:T(8,128)}, f32[512,1024]{1,0:T(8,128)}) fusion(f32[512,1024]{1,0:T(8,128)} %get-tuple-element.8, f32[]{:T(128)} %bitcast.1, f32[512,1024]{1,0:T(8,128)} %get-tuple-element.6), kind=kLoop, calls=%fused_computation | loop fusion | flops 1048576 | bytes 8388612 | tf_op jit(solution)/shard_map/mul | solution.py:901
